TPU v7x, 32 devices: a whole 2x2x4 slice. The times are simulated.
32 devices in a mesh: seq: 8 (over z, y), head: 4 (over x, core).
Axes of the slice: x: 2, y: 2, z: 4, core: 2. Of those that a mesh axis runs over, the one named last changes fastest.
Arguments:
- queries: bfloat16 [4096, 4096], P('seq', 'head'), may hold values from -5 to 5
- keys: bfloat16 [4096, 1024], P('seq', 'head'), may hold values from -5 to 5
- values: bfloat16 [4096, 1024], P('seq', 'head'), may hold values from -5 to 5
- doc_lengths: int32 [16], replicated, may hold values from 1 to 2048, 4096 in all
- out_weight: bfloat16 [4096, 4096], P('head', 'seq'), may hold values from -0.125 to 0.125
Outputs:
- mixed: bfloat16 [4096, 4096], P('seq', 'head')
Inputs may be any that keep to these rules, and one draw needn't show every extreme that they name: `doc_lengths`: the lengths sum to 4096, and one document is exactly 2048 tokens long.
All inputs are finite; a program needn't handle non-finite values.
Results may differ from a plain program's by a relative error of at most 0.012.
Values may be sent and summed in bfloat16 or wider, within the bound.
A program may use at most 128 MiB of HBM per device.

v0:
```python
import math
import jax
import jax.numpy as jnp
from jax import lax
from jax.sharding import PartitionSpec as P

HQ = 32
KV = 8
DH = 128
REACH = 4


def from_behind(block, axis, distance):
    devices = range(lax.axis_size(axis))
    route = [(i - distance, i) for i in devices if i - distance in devices]
    return lax.ppermute(block, axis, route)


def doc_index(positions, starts):
    return jnp.sum((starts[None, :] <= positions[:, None]).astype(jnp.int32), axis=1) - 1


def body(queries, keys, values, doc_lengths, out_weight):
    local_rows = queries.shape[0]
    kv_local = keys.shape[1] // DH
    group_size = HQ // KV
    temper = DH ** (-0.5)
    starts = jnp.cumsum(doc_lengths) - doc_lengths
    q_first = lax.axis_index("seq") * local_rows
    q_pos = q_first + jnp.arange(local_rows, dtype=jnp.int32)
    q_doc = doc_index(q_pos, starts)
    q_heads = queries.reshape(local_rows, kv_local, group_size, DH)

    def attend(carry, piece, piece_start):
        key_piece, value_piece = piece
        key_count = key_piece.shape[0]
        block_len = math.gcd(key_count, 512)
        num_blocks = key_count // block_len
        key_blocks = key_piece.reshape(num_blocks, block_len, kv_local, DH)
        value_blocks = value_piece.reshape(num_blocks, block_len, kv_local, DH)
        block_starts = piece_start + block_len * jnp.arange(num_blocks, dtype=jnp.int32)

        def one_block(state, entry):
            key_block, value_block, block_first = entry
            k_pos = block_first + jnp.arange(block_len, dtype=jnp.int32)
            k_doc = doc_index(k_pos, starts)
            needed = (block_first >= 0) & (block_first <= q_pos[-1]) & (k_doc[-1] >= q_doc[0])

            def update(inner):
                row_max, row_sum, accum = inner
                scores = (
                    jnp.einsum(
                        "qkgd,nkd->kgqn", q_heads, key_block, preferred_element_type=jnp.float32
                    )
                    * temper
                )
                allowed = (k_doc[None, :] == q_doc[:, None]) & (k_pos[None, :] <= q_pos[:, None])
                scores = jnp.where(allowed[None, None], scores, jnp.float32(-1e30))
                new_max = jnp.maximum(row_max, jnp.max(scores, axis=-1))
                probs = jnp.where(
                    allowed[None, None], jnp.exp(scores - new_max[..., None]), jnp.float32(0.0)
                )
                fading = jnp.exp(row_max - new_max)
                row_sum = row_sum * fading + jnp.sum(probs, axis=-1)
                weights = probs.astype(jnp.bfloat16)
                accum = accum * fading[..., None] + jnp.einsum(
                    "kgqn,nkd->kgqd", weights, value_block, preferred_element_type=jnp.float32
                )
                return (new_max, row_sum, accum)

            def unchanged(inner):
                return inner

            return (lax.cond(needed, update, unchanged, state), None)

        carry, _ = lax.scan(one_block, carry, (key_blocks, value_blocks, block_starts))
        return carry

    initial = (
        jnp.full((kv_local, group_size, local_rows), -1e30, jnp.float32),
        jnp.zeros((kv_local, group_size, local_rows), jnp.float32),
        jnp.zeros((kv_local, group_size, local_rows, DH), jnp.float32),
    )
    final = attend(initial, (keys, values), q_first)
    paired = jnp.stack((keys, values))
    for offset in range(REACH):
        paired = from_behind(paired, "seq", 1)
        final = attend(final, (paired[0], paired[1]), q_first - (offset + 1) * local_rows)
    row_max, row_sum, accum = final
    attn = (accum / row_sum[..., None]).astype(jnp.bfloat16)
    attn = jnp.transpose(attn, (2, 0, 1, 3)).reshape(local_rows, kv_local * group_size * DH)
    partial_terms = jnp.dot(
        attn,
        lax.all_gather(out_weight, "seq", axis=1, tiled=True),
        preferred_element_type=jnp.float32,
    )
    return lax.psum_scatter(
        partial_terms.astype(jnp.bfloat16), "head", scatter_dimension=1, tiled=True
    )


def solution(mesh):
    return jax.shard_map(
        body,
        mesh=mesh,
        in_specs=(P("seq", "head"), P("seq", "head"), P("seq", "head"), P(), P("head", "seq")),
        out_specs=P("seq", "head"),
        check_vma=False,
    )
```

profile of v0, /device:TPU:0, one launch (start us, length us, event | category | flops | bytes accessed | tf_op | source)
XLA Modules:
  0.0 233.1 jit_solution(17083058643937626783)
XLA Ops:
  6.5 0.0 all-gather.2.cloned.1.call-start
  6.5 0.7 all-gather.2.cloned.1.call-update
  7.3 0.0 reduce-scatter.2.cloned.1.call-start
  7.3 1.1 copy.53
  8.4 1.1 copy.55
  9.5 0.0 copy-start
  9.5 0.1 pad_maximum_fusion
  9.6 4.9 %collective-permute-start = (bf16[2,512,256]{1,2,0:T(8,128)(2,1)S(1)}, bf16[2,512,256]{1,2,0:T(8,128)(2,1)S(1)}, u32[]{:S(2)}, u32[]{:S(2)}) collective-permute-start(bf16[2,512,256]{1,2,0:T(8,128)(2,1)S(1)} %pad_maximum_fusion), channel_id=1, source_target_pairs={{0,4},{4,8},{8,12},{12,16},{16,20},{20,24},{24,28},{1,5},{5,9},{9,... | collective-permute-start | bytes 1572872 | tf_op jit(solution)/shard_map/ppermute | solution.py:16
  14.5 0.7 copy.52
  15.3 0.1 reduce
  15.4 0.7 sub.95
  16.1 15.3 %collective-permute-done = bf16[2,512,256]{1,2,0:T(8,128)(2,1)S(1)} collective-permute-done((bf16[2,512,256]{1,2,0:T(8,128)(2,1)S(1)}, bf16[2,512,256]{1,2,0:T(8,128)(2,1)S(1)}, u32[]{:S(2)}, u32[]{:S(2)}) %collective-permute-start) | collective-permute-done | bytes 524320 | tf_op jit(solution)/shard_map/ppermute | solution.py:16
  31.4 0.0 copy-start.3
  31.4 4.4 %collective-permute-start.1 = (bf16[2,512,256]{1,2,0:T(8,128)(2,1)S(1)}, bf16[2,512,256]{1,2,0:T(8,128)(2,1)S(1)}, u32[]{:S(2)}, u32[]{:S(2)}) collective-permute-start(bf16[2,512,256]{1,2,0:T(8,128)(2,1)S(1)} %collective-permute-done), channel_id=1, source_target_pairs={{0,4},{4,8},{8,12},{12,16},{16,20},{20,24},{24,28},{1,5},{5,9},{9,... | collective-permute-start | bytes 1572872 | tf_op jit(solution)/shard_map/ppermute | solution.py:16
  35.8 0.1 convert_reduce_fusion
  36.0 12.2 %collective-permute-done.1 = bf16[2,512,256]{1,2,0:T(8,128)(2,1)S(1)} collective-permute-done((bf16[2,512,256]{1,2,0:T(8,128)(2,1)S(1)}, bf16[2,512,256]{1,2,0:T(8,128)(2,1)S(1)}, u32[]{:S(2)}, u32[]{:S(2)}) %collective-permute-start.1) | collective-permute-done | bytes 524320 | tf_op jit(solution)/shard_map/ppermute | solution.py:16
  48.1 0.0 copy-start.2
  48.1 12.2 %collective-permute-start.2 = (bf16[2,512,256]{1,2,0:T(8,128)(2,1)S(1)}, bf16[2,512,256]{1,2,0:T(8,128)(2,1)}, u32[]{:S(2)}, u32[]{:S(2)}) collective-permute-start(bf16[2,512,256]{1,2,0:T(8,128)(2,1)S(1)} %collective-permute-done.1), channel_id=1, source_target_pairs={{0,4},{4,8},{8,12},{12,16},{16,20},{20,24},{24,28},{1,5},{5,9},{9,... | collective-permute-start | bytes 1572872 | tf_op jit(solution)/shard_map/ppermute | solution.py:16
  60.3 6.6 %collective-permute-done.2 = bf16[2,512,256]{1,2,0:T(8,128)(2,1)} collective-permute-done((bf16[2,512,256]{1,2,0:T(8,128)(2,1)S(1)}, bf16[2,512,256]{1,2,0:T(8,128)(2,1)}, u32[]{:S(2)}, u32[]{:S(2)}) %collective-permute-start.2) | collective-permute-done | bytes 524320 | tf_op jit(solution)/shard_map/ppermute | solution.py:16
  66.9 19.1 %collective-permute-start.3 = (bf16[2,512,256]{1,2,0:T(8,128)(2,1)}, bf16[2,512,256]{1,2,0:T(8,128)(2,1)}, u32[]{:S(2)}, u32[]{:S(2)}) collective-permute-start(bf16[2,512,256]{1,2,0:T(8,128)(2,1)} %collective-permute-done.2), channel_id=1, source_target_pairs={{0,4},{4,8},{8,12},{12,16},{16,20},{20,24},{24,28},{1,5},{5,9},{9,... | collective-permute-start | bytes 1572872 | tf_op jit(solution)/shard_map/ppermute | solution.py:16
  86.1 0.6 fusion.68
  86.7 0.6 slice.72
  90.4 0.6 slice.73
  92.2 0.6 slice.75
  93.9 0.7 slice.76
  95.8 0.6 slice.77
  98.7 1.5 copy.54
  100.2 0.0 copy-done
  100.3 0.0 copy-done.3
  100.3 0.0 copy-done.2
  100.3 0.1 broadcast_in_dim.152
  100.4 7.7 %conditional.5 = ((f32[2,4,512]{2,1,0:T(4,128)S(1)}, f32[2,4,512]{2,1,0:T(4,128)S(1)}, f32[2,4,512,128]{3,2,1,0:T(8,128)S(1)})) conditional(s32[]{:T(128)} %convert_element_type.72, (f32[2,4,512]{2,1,0:T(4,128)S(1)}, f32[2,4,512]{2,1,0:T(4,128)S(1)}, f32[2,4,512,128]{3,2,1,0:T(8,128)S(1)}) %tuple.52, (s32[512]{0:T(512)S(1)}, s32[512]{0:T(512)S(1)}, ...), branch_computations={%region_6.7_spmd, %region_7.10_spmd} | conditional | flops 1102848000 | bytes 33296444 | solution.py:74
  100.4 0.3 compare_and_fusion
  100.7 0.0 copy-start.1
  100.7 1.6 fusion
  102.4 2.0 fusion.2
  104.4 0.0 copy-done.1
  104.5 3.6 %multiply_add_fusion = f32[2,4,512,128]{3,2,1,0:T(8,128)S(1)} fusion(f32[2,4,512,128]{3,2,1,0:T(8,128)S(1)} %get-tuple-element.301, f32[2,512,512,4]{2,1,3,0:T(8,128)S(1)} %get-tuple-element.540, f32[2,4,512]{2,1,0:T(4,128)S(1)} %max.11, pred[512,512]{0,1:T(8,128)(4,1)S(1)} %compare_and_fusion, f32[2,4,512]{2,1,0:T(4,128)S(1)} %bitcast.225, ...), kind=kOutput, calls=%fused_computation.7 | convolution fusion | flops 548405248 | bytes 13139968 | tf_op jit(solution)/shard_map/while/body/eval_jaxpr/cond/branch_1_fun/kgqn,nkd->kgqd/dot_general | solution.py:66
  108.1 1.1 fusion.67
  109.2 0.2 conditional.6
  109.4 1.1 fusion.66
  110.5 0.2 conditional.8
  110.7 0.0 collective-permute-done.3
  110.7 1.8 conditional.9
  110.8 1.8 copy.110
  112.6 1.9 divide_convert_fusion
  114.5 53.9 %all-gather.2.cloned.1.call-done = bf16[1024,4096]{1,0:T(8,128)(2,1)} async-done(((bf16[1024,512]{1,0:T(8,128)(2,1)}), bf16[1024,4096]{1,0:T(8,128)(2,1)}) %all-gather.2.cloned.1.call-update) | async-done | bytes 8388624 | tf_op jit(solution)/shard_map/all_gather | solution.py:94
  168.3 9.5 %convolution_convert_fusion = bf16[512,4096]{1,0:T(8,128)(2,1)} fusion(bf16[512,1024]{0,1:T(8,128)(2,1)S(1)} %bitcast.193, bf16[1024,4096]{1,0:T(8,128)(2,1)} %all-gather.2.cloned.1.call-done), kind=kOutput, calls=%fused_computation.81 | convolution fusion | flops 4297064448 | bytes 13631488 | tf_op jit(solution)/shard_map/dot_general | solution.py:92
  177.8 0.0 reduce-scatter.2.cloned.1.call-update
  177.8 48.5 %reduce-scatter.2.cloned.1.call-done = bf16[512,1024]{1,0:T(8,128)(2,1)} async-done(((bf16[512,4096]{1,0:T(8,128)(2,1)}), bf16[512,1024]{1,0:T(8,128)(2,1)}) %reduce-scatter.2.cloned.1.call-update) | async-done | bytes 1048592 | tf_op jit(solution)/shard_map/reduce_scatter | solution.py:97
  (18 shorter events, 0.1 us)
Async XLA Ops:
  6.5 161.8 %all-gather.2.cloned.1.call-start = ((), (), s32[]{:S(2)}) async-start(), calls=%async_computation.1 | async-start | bytes 9437184 | tf_op jit(solution)/shard_map/all_gather | solution.py:94
  7.3 219.1 %reduce-scatter.2.cloned.1.call-start = ((), (), s32[]{:S(2)}) async-start(), calls=%async_computation.2 | async-start | bytes 5242880 | tf_op jit(solution)/shard_map/reduce_scatter | solution.py:97
  9.5 90.7 %copy-start = (bf16[512,256]{0,1:T(8,128)(2,1)}, bf16[512,256]{0,1:T(8,128)(2,1)S(1)}, u32[]{:S(2)}) copy-start(bf16[512,256]{0,1:T(8,128)(2,1)S(1)} %copy.55) | copy-start | bytes 786436
  9.6 21.8 %collective-permute-start = (bf16[2,512,256]{1,2,0:T(8,128)(2,1)S(1)}, bf16[2,512,256]{1,2,0:T(8,128)(2,1)S(1)}, u32[]{:S(2)}, u32[]{:S(2)}) collective-permute-start(bf16[2,512,256]{1,2,0:T(8,128)(2,1)S(1)} %pad_maximum_fusion), channel_id=1, source_target_pairs={{0,4},{4,8},{8,12},{12,16},{16,20},{20,24},{24,28},{1,5},{5,9},{9,... | collective-permute-start | bytes 1572872 | tf_op jit(solution)/shard_map/ppermute | solution.py:16
  31.4 68.9 %copy-start.3 = (bf16[2,512,256]{1,2,0:T(8,128)(2,1)}, bf16[2,512,256]{1,2,0:T(8,128)(2,1)S(1)}, u32[]{:S(2)}) copy-start(bf16[2,512,256]{1,2,0:T(8,128)(2,1)S(1)} %collective-permute-done) | copy-start | bytes 1572868
  31.4 16.7 %collective-permute-start.1 = (bf16[2,512,256]{1,2,0:T(8,128)(2,1)S(1)}, bf16[2,512,256]{1,2,0:T(8,128)(2,1)S(1)}, u32[]{:S(2)}, u32[]{:S(2)}) collective-permute-start(bf16[2,512,256]{1,2,0:T(8,128)(2,1)S(1)} %collective-permute-done), channel_id=1, source_target_pairs={{0,4},{4,8},{8,12},{12,16},{16,20},{20,24},{24,28},{1,5},{5,9},{9,... | collective-permute-start | bytes 1572872 | tf_op jit(solution)/shard_map/ppermute | solution.py:16
  48.1 52.2 %copy-start.2 = (bf16[2,512,256]{1,2,0:T(8,128)(2,1)}, bf16[2,512,256]{1,2,0:T(8,128)(2,1)S(1)}, u32[]{:S(2)}) copy-start(bf16[2,512,256]{1,2,0:T(8,128)(2,1)S(1)} %collective-permute-done.1) | copy-start | bytes 1572868
  48.1 18.8 %collective-permute-start.2 = (bf16[2,512,256]{1,2,0:T(8,128)(2,1)S(1)}, bf16[2,512,256]{1,2,0:T(8,128)(2,1)}, u32[]{:S(2)}, u32[]{:S(2)}) collective-permute-start(bf16[2,512,256]{1,2,0:T(8,128)(2,1)S(1)} %collective-permute-done.1), channel_id=1, source_target_pairs={{0,4},{4,8},{8,12},{12,16},{16,20},{20,24},{24,28},{1,5},{5,9},{9,... | collective-permute-start | bytes 1572872 | tf_op jit(solution)/shard_map/ppermute | solution.py:16
  66.9 43.8 %collective-permute-start.3 = (bf16[2,512,256]{1,2,0:T(8,128)(2,1)}, bf16[2,512,256]{1,2,0:T(8,128)(2,1)}, u32[]{:S(2)}, u32[]{:S(2)}) collective-permute-start(bf16[2,512,256]{1,2,0:T(8,128)(2,1)} %collective-permute-done.2), channel_id=1, source_target_pairs={{0,4},{4,8},{8,12},{12,16},{16,20},{20,24},{24,28},{1,5},{5,9},{9,... | collective-permute-start | bytes 1572872 | tf_op jit(solution)/shard_map/ppermute | solution.py:16
  100.7 3.7 %copy-start.1 = (bf16[512,2,128]{0,2,1:T(8,128)(2,1)S(1)}, bf16[512,2,128]{0,2,1:T(8,128)(2,1)}, u32[]{:S(2)}) copy-start(bf16[512,2,128]{0,2,1:T(8,128)(2,1)} %get-tuple-element.480) | copy-start | bytes 786436 | tf_op jit(solution)/shard_map/while/body/eval_jaxpr/cond
Sparse Core Ops, SparseCore 0:
  9.4 158.9 all-gather.1
  178.0 48.3 reduce-scatter.1
where the time goes:
time: 234 us; the launch traced here: 233 us
  waiting for transfers between devices  137 us (59%)
  starting transfers between devices  40.7 us (17%)
  between operations  22.6 us (10%)
  matrix products  14.7 us (6%)
  local copies, waits for them, and re-layouts  12.2 us (5%)
  other arithmetic  5.23 us (2%)
    all_gather x1, waiting for transfers between devices, body(): lax.all_gather(out_weight, 'seq', axis=1, tiled=True)  53.9 us
    reduce_scatter x1, waiting for transfers between devices, body(): lax.psum_scatter(partial_terms.astype(jnp.bfloat16), 'head', scatter_dime...  48.5 us
    ppermute x4, starting transfers between devices, from_behind(): return lax.ppermute(block, axis, route)  40.7 us
    ppermute x4, waiting for transfers between devices, from_behind(): return lax.ppermute(block, axis, route)  34 us
    dot_general x1, matrix products, body(): jnp.dot(attn, lax.all_gather(out_weight, 'seq', axis=1, tiled=True), pref...  9.46 us
  transfers between devices with their start and end apart: 6, of which 5 were waited for; matrix products, arithmetic and copies ran while one was open for 10% of the time, Pallas kernels for 0%

commit v1 on v0

--- a/solution.py
+++ b/solution.py
@@ -8,6 +8,11 @@
 KV = 8
 DH = 128
 REACH = 4
+
+
+def swapped_in(array, axis, along):
+    repeated = jnp.stack([array] * lax.axis_size(axis))
+    return jnp.concatenate(lax.all_to_all(repeated, axis, 0, 0), axis=along)
 
 
 def from_behind(block, axis, distance):
@@ -90,9 +95,7 @@
     attn = (accum / row_sum[..., None]).astype(jnp.bfloat16)
     attn = jnp.transpose(attn, (2, 0, 1, 3)).reshape(local_rows, kv_local * group_size * DH)
     partial_terms = jnp.dot(
-        attn,
-        lax.all_gather(out_weight, "seq", axis=1, tiled=True),
-        preferred_element_type=jnp.float32,
+        attn, swapped_in(out_weight, "seq", 1), preferred_element_type=jnp.float32
     )
     return lax.psum_scatter(
         partial_terms.astype(jnp.bfloat16), "head", scatter_dimension=1, tiled=True

time: 234 us -> 377 us (1.61); the launches traced: 233 us -> 370 us
  starting transfers between devices: 40.7 us -> 137 us
  waiting for transfers between devices: 137 us -> 166 us
  loops' own time: 0.52 us -> 7.98 us
    ppermute x4, starting transfers between devices: 40.7 us -> 130 us  [from_behind(): return lax.ppermute(block, axis, route)]
    ppermute x4, waiting for transfers between devices: 34 us -> 93.5 us  [from_behind(): return lax.ppermute(block, axis, route)]
    all_gather x1 -> x0, waiting for transfers between devices: 53.9 us -> none  [body(): lax.all_gather(out_weight, 'seq', axis=1, tiled=True)]
    reduce_scatter x1, waiting for transfers between devices: 48.5 us -> 72.5 us  [body(): lax.psum_scatter(partial_terms.astype(jnp.bfloat16), 'head', scatter_dime...]
    another operation x5, loops' own time: 0.52 us -> 7.98 us  [one_block(): return (lax.cond(needed, update, unchanged, state), None)]
    all_to_all x0 -> x1, starting transfers between devices: none -> 7.45 us  [swapped_in(): return jnp.concatenate(lax.all_to_all(repeated, axis, 0, 0), axis=along)]
  transfers between devices with their start and end apart: 6 -> 6, of which waited for: 5 -> 4; matrix products, arithmetic and copies ran while one was open for 10% -> 5% of each run, Pallas kernels for 0% -> 0%
where the time goes in v1:
time: 377 us; the launch traced here: 370 us
  waiting for transfers between devices  166 us (44%)
  starting transfers between devices  137 us (36%)
  between operations  22.9 us (6%)
  local copies, waits for them, and re-layouts  15.9 us (4%)
  matrix products  14.9 us (4%)
  loops' own time  7.98 us (2%)
  other arithmetic  4.56 us (1%)
    ppermute x4, starting transfers between devices, from_behind(): return lax.ppermute(block, axis, route)  130 us
    ppermute x4, waiting for transfers between devices, from_behind(): return lax.ppermute(block, axis, route)  93.5 us
    reduce_scatter x1, waiting for transfers between devices, body(): lax.psum_scatter(partial_terms.astype(jnp.bfloat16), 'head', scatter_dime...  72.5 us
    dot_general x1, matrix products, body(): jnp.dot(attn, swapped_in(out_weight, 'seq', 1), preferred_element_type=jn...  9.63 us
    another operation x5, loops' own time, one_block(): return (lax.cond(needed, update, unchanged, state), None)  7.98 us
  transfers between devices with their start and end apart: 6, of which 4 were waited for; matrix products, arithmetic and copies ran while one was open for 5% of the time, Pallas kernels for 0%

profile of v1, /device:TPU:0, one launch (start us, length us, event | category | flops | bytes accessed | tf_op | source)
XLA Modules:
  0.0 369.6 jit_solution(1898710234335323139)
XLA Ops:
  6.5 1.5 copy.71
  8.0 4.3 %stack.11 = bf16[8,1024,512]{1,2,0:T(8,128)(2,1)} broadcast(bf16[1024,512]{0,1:T(8,128)(2,1)S(1)} %copy.71), dimensions={1,2} | broadcast | bytes 9437184 | tf_op jit(solution)/shard_map/stack | solution.py:14
  12.3 0.0 copy-start.5
  12.3 0.0 copy-start.6
  12.3 0.0 copy-start.9
  12.3 0.0 copy-start
  12.3 7.5 %all-to-all-start = ((bf16[8,1024,512]{1,2,0:T(8,128)(2,1)}), bf16[8,1024,512]{1,2,0:T(8,128)(2,1)}, u32[]{:S(2)}, u32[]{:S(2)}) async-start(bf16[8,1024,512]{1,2,0:T(8,128)(2,1)} %stack.11), calls=%async_computation | async-start | bytes 16777216 | tf_op jit(solution)/shard_map/all_to_all | solution.py:15
  19.8 0.0 reduce-scatter.2.cloned.1.call-start
  19.8 0.0 copy-done.5
  19.8 0.1 copy.54
  20.0 0.0 copy-done.6
  20.0 0.1 copy.56
  20.1 0.0 copy-start.1
  20.2 0.1 pad_maximum_fusion
  20.2 3.9 %collective-permute-start = (bf16[2,512,256]{1,2,0:T(8,128)(2,1)S(1)}, bf16[2,512,256]{1,2,0:T(8,128)(2,1)S(1)}, u32[]{:S(2)}, u32[]{:S(2)}) collective-permute-start(bf16[2,512,256]{1,2,0:T(8,128)(2,1)S(1)} %pad_maximum_fusion), channel_id=1, source_target_pairs={{0,4},{4,8},{8,12},{12,16},{16,20},{20,24},{24,28},{1,5},{5,9},{9,... | collective-permute-start | bytes 1572872 | tf_op jit(solution)/shard_map/ppermute | solution.py:21
  24.2 0.0 copy-done.9
  24.2 0.1 copy.53
  24.3 0.1 reduce
  24.4 75.4 %collective-permute-done = bf16[2,512,256]{1,2,0:T(8,128)(2,1)S(1)} collective-permute-done((bf16[2,512,256]{1,2,0:T(8,128)(2,1)S(1)}, bf16[2,512,256]{1,2,0:T(8,128)(2,1)S(1)}, u32[]{:S(2)}, u32[]{:S(2)}) %collective-permute-start) | collective-permute-done | bytes 524320 | tf_op jit(solution)/shard_map/ppermute | solution.py:21
  99.8 0.0 copy-start.4
  99.8 79.3 %collective-permute-start.1 = (bf16[2,512,256]{1,2,0:T(8,128)(2,1)S(1)}, bf16[2,512,256]{1,2,0:T(8,128)(2,1)S(1)}, u32[]{:S(2)}, u32[]{:S(2)}) collective-permute-start(bf16[2,512,256]{1,2,0:T(8,128)(2,1)S(1)} %collective-permute-done), channel_id=1, source_target_pairs={{0,4},{4,8},{8,12},{12,16},{16,20},{20,24},{24,28},{1,5},{5,9},{9,... | collective-permute-start | bytes 1572872 | tf_op jit(solution)/shard_map/ppermute | solution.py:21
  179.2 0.1 convert_reduce_fusion
  179.3 11.3 %collective-permute-done.1 = bf16[2,512,256]{1,2,0:T(8,128)(2,1)S(1)} collective-permute-done((bf16[2,512,256]{1,2,0:T(8,128)(2,1)S(1)}, bf16[2,512,256]{1,2,0:T(8,128)(2,1)S(1)}, u32[]{:S(2)}, u32[]{:S(2)}) %collective-permute-start.1) | collective-permute-done | bytes 524320 | tf_op jit(solution)/shard_map/ppermute | solution.py:21
  190.6 0.0 copy-start.3
  190.6 13.0 %collective-permute-start.2 = (bf16[2,512,256]{1,2,0:T(8,128)(2,1)S(1)}, bf16[2,512,256]{1,2,0:T(8,128)(2,1)}, u32[]{:S(2)}, u32[]{:S(2)}) collective-permute-start(bf16[2,512,256]{1,2,0:T(8,128)(2,1)S(1)} %collective-permute-done.1), channel_id=1, source_target_pairs={{0,4},{4,8},{8,12},{12,16},{16,20},{20,24},{24,28},{1,5},{5,9},{9,... | collective-permute-start | bytes 1572872 | tf_op jit(solution)/shard_map/ppermute | solution.py:21
  203.7 6.9 %collective-permute-done.2 = bf16[2,512,256]{1,2,0:T(8,128)(2,1)} collective-permute-done((bf16[2,512,256]{1,2,0:T(8,128)(2,1)S(1)}, bf16[2,512,256]{1,2,0:T(8,128)(2,1)}, u32[]{:S(2)}, u32[]{:S(2)}) %collective-permute-start.2) | collective-permute-done | bytes 524320 | tf_op jit(solution)/shard_map/ppermute | solution.py:21
  210.5 33.5 %collective-permute-start.3 = (bf16[2,512,256]{1,2,0:T(8,128)(2,1)}, bf16[2,512,256]{1,2,0:T(8,128)(2,1)}, u32[]{:S(2)}, u32[]{:S(2)}) collective-permute-start(bf16[2,512,256]{1,2,0:T(8,128)(2,1)} %collective-permute-done.2), channel_id=1, source_target_pairs={{0,4},{4,8},{8,12},{12,16},{16,20},{20,24},{24,28},{1,5},{5,9},{9,... | collective-permute-start | bytes 1572872 | tf_op jit(solution)/shard_map/ppermute | solution.py:21
  244.0 0.7 fusion.68
  244.6 0.6 slice.72
  247.9 0.6 slice.76
  248.6 0.6 slice.77
  252.9 0.7 slice.75
  254.8 0.6 slice.73
  256.7 0.0 copy-done.4
  256.7 0.0 copy-done
  256.8 0.5 copy.55
  257.3 0.0 copy-done.1
  257.3 0.0 copy-done.3
  257.3 0.1 broadcast_in_dim.152
  257.5 7.7 %conditional.5 = ((f32[2,4,512]{2,1,0:T(4,128)S(1)}, f32[2,4,512]{2,1,0:T(4,128)S(1)}, f32[2,4,512,128]{3,2,1,0:T(8,128)S(1)})) conditional(s32[]{:T(128)} %convert_element_type.72, (f32[2,4,512]{2,1,0:T(4,128)S(1)}, f32[2,4,512]{2,1,0:T(4,128)S(1)}, f32[2,4,512,128]{3,2,1,0:T(8,128)S(1)}) %tuple.52, (s32[512]{0:T(512)S(1)}, s32[512]{0:T(512)S(1)}, ...), branch_computations={%region_6.7_spmd, %region_7.10_spmd} | conditional | flops 1102848000 | bytes 33296444 | solution.py:79
  257.5 0.3 compare_and_fusion
  257.8 0.0 copy-start.2
  257.8 1.6 fusion
  259.4 2.0 fusion.2
  261.5 0.0 copy-done.2
  261.5 3.6 multiply_add_fusion
  265.2 1.8 fusion.67
  267.0 0.4 conditional.6
  267.4 1.8 fusion.66
  269.2 6.6 %conditional.8 = ((f32[2,4,512]{2,1,0:T(4,128)S(1)}, f32[2,4,512]{2,1,0:T(4,128)S(1)}, f32[2,4,512,128]{3,2,1,0:T(8,128)S(1)})) conditional(s32[]{:T(128)} %convert_element_type.67, (f32[2,4,512]{2,1,0:T(4,128)S(1)}, f32[2,4,512]{2,1,0:T(4,128)S(1)}, f32[2,4,512,128]{3,2,1,0:T(8,128)S(1)}) %get-tuple-element.601, (s32[512]{0:T(512)S(1)}, ...), branch_computations={%region_18.19_spmd, %region_19.22_spmd} | conditional | flops 1102848512 | bytes 33304612 | solution.py:79
  275.8 0.0 collective-permute-done.3
  275.8 2.7 conditional.9
  275.8 1.8 copy.112
  278.5 1.9 divide_convert_fusion
  280.4 0.0 all-to-all-done
  280.4 9.6 %convolution_convert_fusion = bf16[512,4096]{1,0:T(8,128)(2,1)} fusion(bf16[512,1024]{0,1:T(8,128)(2,1)S(1)} %bitcast.196, bf16[1024,4096]{0,1:T(8,128)(2,1)} %bitcast.38), kind=kOutput, calls=%fused_computation.81 | convolution fusion | flops 4297064448 | bytes 13631488 | tf_op jit(solution)/shard_map/dot_general | solution.py:97
  290.0 0.0 reduce-scatter.2.cloned.1.call-update
  290.0 72.5 %reduce-scatter.2.cloned.1.call-done = bf16[512,1024]{1,0:T(8,128)(2,1)} async-done(((bf16[512,4096]{1,0:T(8,128)(2,1)}), bf16[512,1024]{1,0:T(8,128)(2,1)}) %reduce-scatter.2.cloned.1.call-update) | async-done | bytes 1048592 | tf_op jit(solution)/shard_map/reduce_scatter | solution.py:100
  (19 shorter events, 0.1 us)
Async XLA Ops:
  12.3 7.5 %copy-start.5 = (bf16[512,256]{1,0:T(8,128)(2,1)S(1)}, bf16[512,256]{1,0:T(8,128)(2,1)}, u32[]{:S(2)}) copy-start(bf16[512,256]{1,0:T(8,128)(2,1)} %param.16) | copy-start | bytes 786436
  12.3 7.7 %copy-start.6 = (bf16[512,256]{1,0:T(8,128)(2,1)S(1)}, bf16[512,256]{1,0:T(8,128)(2,1)}, u32[]{:S(2)}) copy-start(bf16[512,256]{1,0:T(8,128)(2,1)} %param.17) | copy-start | bytes 786436
  12.3 11.8 %copy-start.9 = (s32[16]{0:T(128)S(1)}, s32[16]{0:T(128)}, u32[]{:S(2)}) copy-start(s32[16]{0:T(128)} %param.18) | copy-start | bytes 196
  12.3 244.4 %copy-start = (bf16[512,1024]{1,0:T(8,128)(2,1)S(1)}, bf16[512,1024]{1,0:T(8,128)(2,1)}, u32[]{:S(2)}) copy-start(bf16[512,1024]{1,0:T(8,128)(2,1)} %param.15) | copy-start | bytes 3145732
  12.3 268.0 %all-to-all-start = ((bf16[8,1024,512]{1,2,0:T(8,128)(2,1)}), bf16[8,1024,512]{1,2,0:T(8,128)(2,1)}, u32[]{:S(2)}, u32[]{:S(2)}) async-start(bf16[8,1024,512]{1,2,0:T(8,128)(2,1)} %stack.11), calls=%async_computation | async-start | bytes 16777216 | tf_op jit(solution)/shard_map/all_to_all | solution.py:15
  19.8 342.8 %reduce-scatter.2.cloned.1.call-start = ((), (), s32[]{:S(2)}) async-start(), calls=%async_computation.2 | async-start | bytes 5242880 | tf_op jit(solution)/shard_map/reduce_scatter | solution.py:100
  20.1 237.2 %copy-start.1 = (bf16[512,256]{0,1:T(8,128)(2,1)}, bf16[512,256]{0,1:T(8,128)(2,1)S(1)}, u32[]{:S(2)}) copy-start(bf16[512,256]{0,1:T(8,128)(2,1)S(1)} %copy.56) | copy-start | bytes 786436
  20.2 79.6 %collective-permute-start = (bf16[2,512,256]{1,2,0:T(8,128)(2,1)S(1)}, bf16[2,512,256]{1,2,0:T(8,128)(2,1)S(1)}, u32[]{:S(2)}, u32[]{:S(2)}) collective-permute-start(bf16[2,512,256]{1,2,0:T(8,128)(2,1)S(1)} %pad_maximum_fusion), channel_id=1, source_target_pairs={{0,4},{4,8},{8,12},{12,16},{16,20},{20,24},{24,28},{1,5},{5,9},{9,... | collective-permute-start | bytes 1572872 | tf_op jit(solution)/shard_map/ppermute | solution.py:21
  99.8 156.9 %copy-start.4 = (bf16[2,512,256]{1,2,0:T(8,128)(2,1)}, bf16[2,512,256]{1,2,0:T(8,128)(2,1)S(1)}, u32[]{:S(2)}) copy-start(bf16[2,512,256]{1,2,0:T(8,128)(2,1)S(1)} %collective-permute-done) | copy-start | bytes 1572868
  99.8 90.8 %collective-permute-start.1 = (bf16[2,512,256]{1,2,0:T(8,128)(2,1)S(1)}, bf16[2,512,256]{1,2,0:T(8,128)(2,1)S(1)}, u32[]{:S(2)}, u32[]{:S(2)}) collective-permute-start(bf16[2,512,256]{1,2,0:T(8,128)(2,1)S(1)} %collective-permute-done), channel_id=1, source_target_pairs={{0,4},{4,8},{8,12},{12,16},{16,20},{20,24},{24,28},{1,5},{5,9},{9,... | collective-permute-start | bytes 1572872 | tf_op jit(solution)/shard_map/ppermute | solution.py:21
  190.6 66.7 %copy-start.3 = (bf16[2,512,256]{1,2,0:T(8,128)(2,1)}, bf16[2,512,256]{1,2,0:T(8,128)(2,1)S(1)}, u32[]{:S(2)}) copy-start(bf16[2,512,256]{1,2,0:T(8,128)(2,1)S(1)} %collective-permute-done.1) | copy-start | bytes 1572868
  190.6 19.9 %collective-permute-start.2 = (bf16[2,512,256]{1,2,0:T(8,128)(2,1)S(1)}, bf16[2,512,256]{1,2,0:T(8,128)(2,1)}, u32[]{:S(2)}, u32[]{:S(2)}) collective-permute-start(bf16[2,512,256]{1,2,0:T(8,128)(2,1)S(1)} %collective-permute-done.1), channel_id=1, source_target_pairs={{0,4},{4,8},{8,12},{12,16},{16,20},{20,24},{24,28},{1,5},{5,9},{9,... | collective-permute-start | bytes 1572872 | tf_op jit(solution)/shard_map/ppermute | solution.py:21
  210.5 65.3 %collective-permute-start.3 = (bf16[2,512,256]{1,2,0:T(8,128)(2,1)}, bf16[2,512,256]{1,2,0:T(8,128)(2,1)}, u32[]{:S(2)}, u32[]{:S(2)}) collective-permute-start(bf16[2,512,256]{1,2,0:T(8,128)(2,1)} %collective-permute-done.2), channel_id=1, source_target_pairs={{0,4},{4,8},{8,12},{12,16},{16,20},{20,24},{24,28},{1,5},{5,9},{9,... | collective-permute-start | bytes 1572872 | tf_op jit(solution)/shard_map/ppermute | solution.py:21
  257.8 3.7 %copy-start.2 = (bf16[512,2,128]{0,2,1:T(8,128)(2,1)S(1)}, bf16[512,2,128]{0,2,1:T(8,128)(2,1)}, u32[]{:S(2)}) copy-start(bf16[512,2,128]{0,2,1:T(8,128)(2,1)} %get-tuple-element.480) | copy-start | bytes 786436 | tf_op jit(solution)/shard_map/while/body/eval_jaxpr/cond
Sparse Core Ops, SparseCore 0:
  290.2 72.3 reduce-scatter.1
